TPU v7x, 128 devices: a whole 4x4x4 slice. The times are simulated.
128 devices in a mesh: grp: 4 (over x), tile: 32 (over y, z, core).
Axes of the slice: x: 4, y: 4, z: 4, core: 2. Of those that a mesh axis runs over, the one named last changes fastest.
Arguments:
- descriptors: bfloat16 [64, 4096, 256], P('grp', 'tile'), may hold values from -8 to 8
- pairs: int32 [32, 2], P('grp'), may hold values from 0 to 63, as said below
- counts: int32 [64], replicated, may hold values from 1024 to 4096
Outputs:
- row_lse: float32 [32, 4096], P('grp', 'tile')
- col_lse: float32 [32, 4096], P('grp', 'tile')
- best_log: float32 [32, 4096], P('grp', 'tile')
Inputs may be any that keep to these rules, and one draw needn't show every extreme that they name: `pairs`: the two images of a pair differ.
All inputs are finite; a program needn't handle non-finite values.
Results may differ from a plain program's by a relative error of at most 0.0003.
Values may be sent and summed in bfloat16 or wider, within the bound.
A program may use at most 64 MiB of HBM per device.

v0:
```python
import math
import jax
import jax.numpy as jnp
from jax import lax
from jax.sharding import Mesh
from jax.sharding import PartitionSpec as P

QBLK = 4
TILE = ("tile_0", "tile_1", "tile_2")
NEGATIVE = -1e30


def in_one_piece(arrays, axis, split_dim, concat_dim, along):
    both = jnp.concatenate(arrays, axis=along)
    out, at, outs = (
        lax.all_to_all(both, axis, split_axis=split_dim, concat_axis=concat_dim, tiled=True),
        0,
        [],
    )
    for a in arrays:
        outs.append(lax.slice_in_dim(out, at, at + a.shape[along], axis=along))
        at += a.shape[along]
    return tuple(outs)


def in_blocks(value, dim, count):
    lengths = value.shape
    tiles = value.reshape(*lengths[:dim], count, lengths[dim] // count, *lengths[dim + 1 :])
    return jnp.moveaxis(tiles, dim, 0)


def joined_along(tiles, dim):
    lengths = list(tiles.shape[1:])
    lengths[dim] *= tiles.shape[0]
    return jnp.moveaxis(tiles, 0, dim).reshape(lengths)


def exchange_in_order(tiles, axes, turns):
    inside = tiles.shape[1:]
    out = tiles.reshape(*(lax.axis_size(a) for a in axes), *inside)
    for k in turns:
        out = lax.all_to_all(out, axes[k], k, k, tiled=True)
    return out.reshape(-1, *inside)


def core_and_chips(value, groups, turns, split_dim, concat_dim):
    count = lax.axis_size(groups[0]) * lax.axis_size(groups[1])
    tiles = in_blocks(value, split_dim, count)
    return joined_along(exchange_in_order(tiles, groups, turns), concat_dim)


def join_stats(earlier, later):
    highest = jnp.maximum(earlier[0], later[0])
    summed = earlier[1] * jnp.exp(earlier[0] - highest) + later[1] * jnp.exp(later[0] - highest)
    return (highest, summed)


def slot_first(item, query_index, score_scale):
    query_rows, key_image, query_count, key_count = item
    height = query_rows.shape[0]
    width = query_rows.shape[1]
    total_keys = key_image.shape[0]
    block = min(512, height)
    number = height // block
    key_mask = (lax.iota(jnp.int32, total_keys) < key_count)[None, :]
    grouped = query_rows.reshape(number, block, width)
    index_groups = query_index.reshape(number, block)

    def first_pass(carried, inputs):
        block_rows, block_index = inputs
        scores = (
            jnp.einsum("qd,kd->qk", block_rows, key_image, preferred_element_type=jnp.float32)
            * score_scale
        )
        query_mask = (block_index < query_count)[:, None]
        row_top = jnp.max(jnp.where(key_mask, scores, NEGATIVE), axis=1)
        row_total = jnp.sum(jnp.where(key_mask, jnp.exp(scores - row_top[:, None]), 0.0), axis=1)
        col_top = jnp.max(jnp.where(query_mask, scores, NEGATIVE), axis=0)
        col_total = jnp.sum(jnp.where(query_mask, jnp.exp(scores - col_top[None, :]), 0.0), axis=0)
        return (join_stats(carried, (col_top, col_total)), row_top + jnp.log(row_total))

    start_stats = (
        jnp.full((total_keys,), NEGATIVE, jnp.float32),
        jnp.zeros((total_keys,), jnp.float32),
    )
    col_stats, row_values = lax.scan(first_pass, start_stats, (grouped, index_groups))
    return (col_stats[0], col_stats[1], row_values.reshape(height))


def slot_second(item, query_index, score_scale):
    query_rows, key_image, row_values, col_values, query_count, key_count = item
    height = query_rows.shape[0]
    width = query_rows.shape[1]
    total_keys = key_image.shape[0]
    block = min(512, height)
    number = height // block
    key_mask = (lax.iota(jnp.int32, total_keys) < key_count)[None, :]
    grouped = query_rows.reshape(number, block, width)
    lse_groups = row_values.reshape(number, block)

    def second_pass(carried, inputs):
        block_rows, block_lse = inputs
        scores = (
            jnp.einsum("qd,kd->qk", block_rows, key_image, preferred_element_type=jnp.float32)
            * score_scale
        )
        best = (
            jnp.max(jnp.where(key_mask, 2.0 * scores - col_values[None, :], NEGATIVE), axis=1)
            - block_lse
        )
        return (carried, best)

    unused, best_values = lax.scan(second_pass, jnp.int32(0), (grouped, lse_groups))
    query_valid = query_index < query_count
    return (
        jnp.where(query_valid, row_values, 0.0),
        jnp.where(query_valid, best_values.reshape(height), 0.0),
    )


def paired_blocks(queries, keys_local, query_counts, key_counts, score_scale):
    devices_here = lax.axis_size(TILE)
    rows = queries.shape[1]
    width = queries.shape[2]
    slots = devices_here // QBLK
    sub = rows // QBLK
    pair_count = queries.shape[0]
    per_slot = -(-pair_count // slots)
    padded = per_slot * slots
    query_send = (
        queries.reshape(slots, per_slot, QBLK, sub, width)
        .transpose(0, 2, 1, 3, 4)
        .reshape(devices_here, per_slot, sub, width)
    )
    key_send = jnp.broadcast_to(
        keys_local.reshape(slots, 1, per_slot, rows, width), (slots, QBLK, per_slot, rows, width)
    ).reshape(devices_here, per_slot, rows, width)
    query_got, key_got = in_one_piece((query_send, key_send), TILE, 0, 0, 2)
    query_here = query_got.transpose(1, 0, 2, 3).reshape(per_slot, devices_here * sub, width)
    key_here = key_got.transpose(1, 0, 2, 3).reshape(per_slot, devices_here * rows, width)
    place = lax.axis_index(TILE)
    slot = place // QBLK
    quarter = place % QBLK
    query_index = (
        lax.iota(jnp.int32, devices_here)[:, None] * rows
        + quarter * sub
        + lax.iota(jnp.int32, sub)[None, :]
    ).reshape(devices_here * sub)
    query_own = lax.dynamic_slice_in_dim(query_counts, slot * per_slot, per_slot, 0)
    key_own = lax.dynamic_slice_in_dim(key_counts, slot * per_slot, per_slot, 0)
    col_top, col_total, row_values = lax.map(
        lambda item: slot_first(item, query_index, score_scale),
        (query_here, key_here, query_own, key_own),
    )

    def by_block(values):
        return values.reshape(per_slot, devices_here, rows).transpose(1, 0, 2)

    top_got, total_got = in_one_piece((by_block(col_top), by_block(col_total)), TILE, 0, 0, 1)
    top_got = top_got.reshape(slots, QBLK, per_slot, rows)
    total_got = total_got.reshape(slots, QBLK, per_slot, rows)
    stats = (top_got[:, 0], total_got[:, 0])
    for member in range(1, QBLK):
        stats = join_stats(stats, (top_got[:, member], total_got[:, member]))
    col_block = stats[0] + jnp.log(stats[1])
    col_send = jnp.broadcast_to(col_block[:, None], (slots, QBLK, per_slot, rows)).reshape(
        devices_here, per_slot, rows
    )
    col_got = core_and_chips(col_send, (("tile_0", "tile_1"), "tile_2"), (1, 0), 0, 0)
    col_values = col_got.transpose(1, 0, 2).reshape(per_slot, devices_here * rows)
    row_out, best_out = lax.map(
        lambda item: slot_second(item, query_index, score_scale),
        (query_here, key_here, row_values, col_values, query_own, key_own),
    )

    def to_owner(values):
        return values.reshape(per_slot, devices_here, sub).transpose(1, 0, 2)

    row_got, best_got = (
        lax.all_to_all(to_owner(row_out), TILE, split_axis=0, concat_axis=0, tiled=True),
        lax.all_to_all(to_owner(best_out), TILE, split_axis=0, concat_axis=0, tiled=True),
    )

    def from_slots(values):
        return (
            values.reshape(slots, QBLK, per_slot, sub).transpose(0, 2, 1, 3).reshape(padded, rows)
        )

    key_place = place * rows + lax.iota(jnp.int32, rows)
    key_valid_own = key_place[None, :] < key_counts[:, None]
    col_out = jnp.where(key_valid_own, col_block.reshape(padded, rows), 0.0)
    return (from_slots(row_got), col_out, from_slots(best_got))


def local(descriptors, pairs, counts):
    score_scale = 2.0 / math.sqrt(descriptors.shape[2])
    image_rows = lax.all_gather(descriptors, "grp", axis=0, tiled=True)
    image_ids = lax.iota(jnp.int32, counts.shape[0])
    first_image = pairs[:, 0]
    second = pairs[:, 1]
    query_counts = jnp.sum(
        jnp.where(first_image[:, None] == image_ids[None, :], counts[None, :], 0), axis=1
    )
    key_counts = jnp.sum(
        jnp.where(second[:, None] == image_ids[None, :], counts[None, :], 0), axis=1
    )
    queries = jnp.take(image_rows, first_image, axis=0)
    keys_local = jnp.take(image_rows, second, axis=0)
    return paired_blocks(queries, keys_local, query_counts, key_counts, score_scale)


def solution(mesh):
    torus = Mesh(
        mesh.devices.reshape(mesh.shape["grp"], 4, 4, 2), ("grp", "tile_0", "tile_1", "tile_2")
    )
    return jax.shard_map(
        local,
        mesh=torus,
        in_specs=(P("grp", TILE, None), P("grp", None), P()),
        out_specs=(P("grp", TILE), P("grp", TILE), P("grp", TILE)),
        check_vma=False,
    )
```

profile of v0, /device:TPU:1, one launch (start us, length us, event | category | flops | bytes accessed | tf_op | source)
XLA Modules:
  0.0 198.5 jit_solution(10425971025592148428)
XLA Ops:
  7.2 0.0 all-gather.2.cloned.1.call-start
  7.2 0.7 all-gather.2.cloned.1.call-update
  7.9 0.8 compare_and_fusion.1
  8.7 52.2 %all-gather.2.cloned.1.call-done = bf16[64,128,256]{2,1,0:T(8,128)(2,1)} async-done(((bf16[16,128,256]{2,1,0:T(8,128)(2,1)}), bf16[64,128,256]{2,1,0:T(8,128)(2,1)}) %all-gather.2.cloned.1.call-update) | async-done | bytes 4194320 | tf_op jit(solution)/shard_map/all_gather | solution.py:197
  60.9 2.8 %gather_fusion = bf16[8,128,256]{2,1,0:T(8,128)(2,1)S(1)} fusion(bf16[64,128,256]{2,1,0:T(8,128)(2,1)} %all-gather.2.cloned.1.call-done, s32[1024]{0:T(1024)S(1)} %pad_clamp_fusion.1), kind=kCustom, calls=%fused_computation.clone | custom fusion | bytes 1048608 | tf_op jit(solution)/shard_map/jit(_take)/gather | solution.py:207
  63.6 0.0 copy-start
  63.7 0.0 copy-start.1
  63.7 2.8 %gather_fusion.1 = bf16[8,128,256]{2,1,0:T(8,128)(2,1)S(1)} fusion(bf16[64,128,256]{2,1,0:T(8,128)(2,1)} %all-gather.2.cloned.1.call-done, s32[1024]{0:T(1024)S(1)} %pad_clamp_fusion), kind=kCustom, calls=%fused_computation.1.clone | custom fusion | bytes 1048608 | tf_op jit(solution)/shard_map/jit(_take)/gather | solution.py:208
  66.5 0.2 broadcast_select_fusion
  66.6 0.2 broadcast_in_dim.140
  66.9 1.7 pad_maximum_fusion
  68.6 7.9 %all-to-all-start = ((bf16[32,1,160,256]{3,2,1,0:T(8,128)(2,1)}), bf16[32,1,160,256]{3,2,1,0:T(8,128)(2,1)S(1)}, u32[]{:S(2)}, u32[]{:S(2)}) async-start(bf16[32,1,160,256]{3,2,1,0:T(8,128)(2,1)} %pad_maximum_fusion), calls=%async_computation | async-start | bytes 5242880 | tf_op jit(solution)/shard_map/all_to_all | solution.py:16
  76.5 0.0 copy-done
  76.5 0.0 copy-done.1
  76.5 0.2 select_reduce_fusion.5
  76.8 0.6 dynamic_slice.52
  77.4 0.6 dynamic_slice.53
  77.9 0.1 add.159
  78.0 0.1 add.160
  78.1 0.1 add.162
  78.2 32.2 %all-to-all-done = bf16[32,1,160,256]{3,2,1,0:T(8,128)(2,1)S(1)} async-done(((bf16[32,1,160,256]{3,2,1,0:T(8,128)(2,1)}), bf16[32,1,160,256]{3,2,1,0:T(8,128)(2,1)S(1)}, u32[]{:S(2)}, u32[]{:S(2)}) %all-to-all-start) | async-done | bytes 2621472 | tf_op jit(solution)/shard_map/all_to_all | solution.py:16
  110.4 1.5 slice.61
  112.0 20.6 %while.48 = (s32[]{:T(128)}, f32[4096]{0:T(1024)S(1)}, f32[4096]{0:T(1024)S(1)}, f32[2,512]{1,0:T(2,128)S(1)}, s32[2,512]{1,0:T(2,128)S(1)}, /*index=5*/s32[]{:T...) while((s32[]{:T(128)}, f32[4096]{0:T(1024)S(1)}, ...), condition=%wide.region_7.9_spmd.clone, body=%wide.region_2.8_spmd.clone.sunk | while | flops 1098936320 | bytes 19316360 | solution.py:86
  112.0 0.7 compare_reduce_fusion.8
  112.6 0.7 compare_reduce_fusion.7
  113.3 4.0 %select_reduce_fusion.11 = (f32[512]{0:T(512)S(1)}, f32[4096]{0:T(1024)S(1)}, f32[512,4096]{1,0:T(8,128)S(1)}) fusion(pred[4096]{0:T(1024)(128)(4,1)S(1)} %compare_reduce_fusion.7, pred[512]{0:T(512)(128)(4,1)S(1)} %compare_reduce_fusion.8, bf16[4096,256]{1,0:T(8,128)(2,1)} %get-tuple-element.457, bf16[2,512,256]{2,1,0:T(8,128)(2,1)S(1)} %get-tuple-element.456, ...), kind=kOutput, calls=%fused_computation.11.clone.1 | convolution fusion | flops 1084222976 | bytes 10770948 | tf_op jit(solution)/shard_map/while/body/eval_jaxpr/while/body/eval_jaxpr/qd,kd->qk/dot_general | solution.py:72
  117.3 4.8 %select_reduce_fusion.12 = (f32[512]{0:T(512)S(1)}, f32[4096]{0:T(1024)S(1)}) fusion(f32[512,4096]{1,0:T(8,128)S(1)} %get-tuple-element.421, f32[512]{0:T(512)S(1)} %get-tuple-element.422, pred[4096]{0:T(1024)(128)(4,1)S(1)} %compare_reduce_fusion.7, f32[4096]{0:T(1024)S(1)} %get-tuple-element.423, pred[512]{0:T(512)(128)(4,1)S(1)} %compare_reduce_fusion.8), kind=kLoop, calls=%fused_computation.10.clone.1 | loop fusion | flops 14675456 | bytes 8430080 | tf_op jit(solution)/shard_map/while/body/eval_jaxpr/while/body/eval_jaxpr/reduce_sum | solution.py:77
  122.3 0.7 compare_reduce_fusion.8
  122.9 0.7 compare_reduce_fusion.7
  123.6 3.9 %select_reduce_fusion.11 = (f32[512]{0:T(512)S(1)}, f32[4096]{0:T(1024)S(1)}, f32[512,4096]{1,0:T(8,128)S(1)}) fusion(pred[4096]{0:T(1024)(128)(4,1)S(1)} %compare_reduce_fusion.7, pred[512]{0:T(512)(128)(4,1)S(1)} %compare_reduce_fusion.8, bf16[4096,256]{1,0:T(8,128)(2,1)} %get-tuple-element.457, bf16[2,512,256]{2,1,0:T(8,128)(2,1)S(1)} %get-tuple-element.456, ...), kind=kOutput, calls=%fused_computation.11.clone.1 | convolution fusion | flops 1084222976 | bytes 10770948 | tf_op jit(solution)/shard_map/while/body/eval_jaxpr/while/body/eval_jaxpr/qd,kd->qk/dot_general | solution.py:72
  127.6 4.8 %select_reduce_fusion.12 = (f32[512]{0:T(512)S(1)}, f32[4096]{0:T(1024)S(1)}) fusion(f32[512,4096]{1,0:T(8,128)S(1)} %get-tuple-element.421, f32[512]{0:T(512)S(1)} %get-tuple-element.422, pred[4096]{0:T(1024)(128)(4,1)S(1)} %compare_reduce_fusion.7, f32[4096]{0:T(1024)S(1)} %get-tuple-element.423, pred[512]{0:T(512)(128)(4,1)S(1)} %compare_reduce_fusion.8), kind=kLoop, calls=%fused_computation.10.clone.1 | loop fusion | flops 14675456 | bytes 8430080 | tf_op jit(solution)/shard_map/while/body/eval_jaxpr/while/body/eval_jaxpr/reduce_sum | solution.py:77
  132.6 11.1 %all_to_all.30 = f32[32,2,128]{2,1,0:T(2,128)S(1)} all-to-all(f32[32,2,128]{2,1,0:T(2,128)S(1)} %pad_maximum_fusion.1), channel_id=1, replica_groups=mesh['grp'=4,'tile_0'=4,'tile_1'=4,'tile_2'=2] {'tile_0','tile_1','tile_2'}, dimensions={0} | all-to-all | bytes 65536 | tf_op jit(solution)/shard_map/all_to_all | solution.py:16
  143.8 3.8 %all_to_all.31 = f32[16,2,1,1,128]{4,3,2,0,1:T(1,128)S(1)} all-to-all(f32[16,2,1,1,128]{4,3,2,0,1:T(1,128)S(1)} %broadcast_in_dim.147), channel_id=1, replica_groups=mesh['grp'=4,'tile_0'=4,'tile_1'=4,'tile_2'=2] {'tile_2'}, dimensions={1} | all-to-all | bytes 32768 | tf_op jit(solution)/shard_map/all_to_all | solution.py:42
  147.5 0.6 copy.107
  148.1 3.5 %all-to-all-start.4 = ((f32[16,2,1,1,128]{4,3,2,1,0:T(1,128)}), f32[16,2,1,1,128]{4,3,2,1,0:T(1,128)S(1)}, u32[]{:S(2)}, u32[]{:S(2)}) async-start(f32[16,2,1,1,128]{4,3,2,1,0:T(1,128)} %copy.107), calls=%async_computation.4 | async-start | bytes 32768 | tf_op jit(solution)/shard_map/all_to_all | solution.py:42
  151.7 0.1 squeeze.81
  151.8 6.3 %all-to-all-done.4 = f32[16,2,1,1,128]{4,3,2,1,0:T(1,128)S(1)} async-done(((f32[16,2,1,1,128]{4,3,2,1,0:T(1,128)}), f32[16,2,1,1,128]{4,3,2,1,0:T(1,128)S(1)}, u32[]{:S(2)}, u32[]{:S(2)}) %all-to-all-start.4) | async-done | bytes 16416 | tf_op jit(solution)/shard_map/all_to_all | solution.py:42
  158.0 7.6 %while.47 = (s32[]{:T(128)}, f32[2,512]{1,0:T(2,128)S(1)}, bf16[2,512,256]{2,1,0:T(8,128)(2,1)S(1)}, bf16[4096,256]{1,0:T(8,128)(2,1)}, f32[4096]{0:T(1024)S(1)}...) while((s32[]{:T(128)}, f32[2,512]{1,0:T(2,128)S(1)}, ...), condition=%wide.region_10.12_spmd.clone, body=%wide.region_8.11_spmd.clone.sunk | while | flops 1082134528 | bytes 2396269 | solution.py:113
  158.0 0.7 compare_reduce_fusion.6
  158.7 3.0 %select_reduce_fusion.10 = f32[512]{0:T(512)S(1)} fusion(bf16[4096,256]{1,0:T(8,128)(2,1)} %get-tuple-element.482, f32[4096]{0:T(1024)S(1)} %get-tuple-element.483, pred[4096]{0:T(1024)(128)(4,1)S(1)} %compare_reduce_fusion.6, bf16[2,512,256]{2,1,0:T(8,128)(2,1)S(1)} %get-tuple-element.481, s32[]{:T(128)} %get-tuple-element.470), kind=kOutput, calls=%fused_computation.4.clone.1 | convolution fusion | flops 1082129920 | bytes 2381828 | tf_op jit(solution)/shard_map/while/body/eval_jaxpr/while/body/eval_jaxpr/qd,kd->qk/dot_general | solution.py:104
  161.8 0.7 compare_reduce_fusion.6
  162.5 3.0 %select_reduce_fusion.10 = f32[512]{0:T(512)S(1)} fusion(bf16[4096,256]{1,0:T(8,128)(2,1)} %get-tuple-element.482, f32[4096]{0:T(1024)S(1)} %get-tuple-element.483, pred[4096]{0:T(1024)(128)(4,1)S(1)} %compare_reduce_fusion.6, bf16[2,512,256]{2,1,0:T(8,128)(2,1)S(1)} %get-tuple-element.481, s32[]{:T(128)} %get-tuple-element.470), kind=kOutput, calls=%fused_computation.4.clone.1 | convolution fusion | flops 1082129920 | bytes 2381828 | tf_op jit(solution)/shard_map/while/body/eval_jaxpr/while/body/eval_jaxpr/qd,kd->qk/dot_general | solution.py:104
  165.6 0.1 reshape.246
  165.7 1.4 compare_select_fusion
  167.1 4.9 %all-to-all-start.1 = ((f32[32,1,32]{2,1,0:T(1,128)}), f32[32,1,32]{2,1,0:T(1,128)S(1)}, u32[]{:S(2)}, u32[]{:S(2)}) async-start(f32[32,1,32]{2,1,0:T(1,128)} %get-tuple-element.313), calls=%async_computation.1 | async-start | bytes 32768 | tf_op jit(solution)/shard_map/all_to_all | solution.py:180
  172.0 7.1 %all-to-all-done.1 = f32[32,1,32]{2,1,0:T(1,128)S(1)} async-done(((f32[32,1,32]{2,1,0:T(1,128)}), f32[32,1,32]{2,1,0:T(1,128)S(1)}, u32[]{:S(2)}, u32[]{:S(2)}) %all-to-all-start.1) | async-done | bytes 4128 | tf_op jit(solution)/shard_map/all_to_all | solution.py:180
  179.1 4.2 %all-to-all-start.5 = ((f32[32,1,32]{2,1,0:T(1,128)}), f32[32,1,32]{2,1,0:T(1,128)S(1)}, u32[]{:S(2)}, u32[]{:S(2)}) async-start(f32[32,1,32]{2,1,0:T(1,128)} %get-tuple-element.312), calls=%async_computation.5 | async-start | bytes 32768 | tf_op jit(solution)/shard_map/all_to_all | solution.py:181
  183.2 0.7 add_select_fusion
  183.9 0.5 broadcast.199
  184.4 0.7 reduce.12
  185.1 0.7 reshape_transpose_reshape.10
  185.8 4.5 %all-to-all-done.5 = f32[32,1,32]{2,1,0:T(1,128)S(1)} async-done(((f32[32,1,32]{2,1,0:T(1,128)}), f32[32,1,32]{2,1,0:T(1,128)S(1)}, u32[]{:S(2)}, u32[]{:S(2)}) %all-to-all-start.5) | async-done | bytes 4128 | tf_op jit(solution)/shard_map/all_to_all | solution.py:181
  190.3 0.7 reduce.13
  191.0 0.7 reshape_transpose_reshape.11
  (30 shorter events, 0.5 us)
Async XLA Ops:
  7.2 53.7 %all-gather.2.cloned.1.call-start = ((), (), s32[]{:S(2)}) async-start(), calls=%async_computation.6 | async-start | bytes 5242880 | tf_op jit(solution)/shard_map/all_gather | solution.py:197
  63.6 12.9 %copy-start = (s32[8,2]{0,1:T(2,128)S(1)}, s32[8,2]{0,1:T(2,128)}, u32[]{:S(2)}) copy-start(s32[8,2]{0,1:T(2,128)} %param.10) | copy-start | bytes 196
  63.7 12.9 %copy-start.1 = (s32[64]{0:T(128)S(1)}, s32[64]{0:T(128)}, u32[]{:S(2)}) copy-start(s32[64]{0:T(128)} %param.11) | copy-start | bytes 772
  68.6 41.8 %all-to-all-start = ((bf16[32,1,160,256]{3,2,1,0:T(8,128)(2,1)}), bf16[32,1,160,256]{3,2,1,0:T(8,128)(2,1)S(1)}, u32[]{:S(2)}, u32[]{:S(2)}) async-start(bf16[32,1,160,256]{3,2,1,0:T(8,128)(2,1)} %pad_maximum_fusion), calls=%async_computation | async-start | bytes 5242880 | tf_op jit(solution)/shard_map/all_to_all | solution.py:16
  148.1 9.9 %all-to-all-start.4 = ((f32[16,2,1,1,128]{4,3,2,1,0:T(1,128)}), f32[16,2,1,1,128]{4,3,2,1,0:T(1,128)S(1)}, u32[]{:S(2)}, u32[]{:S(2)}) async-start(f32[16,2,1,1,128]{4,3,2,1,0:T(1,128)} %copy.107), calls=%async_computation.4 | async-start | bytes 32768 | tf_op jit(solution)/shard_map/all_to_all | solution.py:42
  167.1 12.0 %all-to-all-start.1 = ((f32[32,1,32]{2,1,0:T(1,128)}), f32[32,1,32]{2,1,0:T(1,128)S(1)}, u32[]{:S(2)}, u32[]{:S(2)}) async-start(f32[32,1,32]{2,1,0:T(1,128)} %get-tuple-element.313), calls=%async_computation.1 | async-start | bytes 32768 | tf_op jit(solution)/shard_map/all_to_all | solution.py:180
  179.1 11.2 %all-to-all-start.5 = ((f32[32,1,32]{2,1,0:T(1,128)}), f32[32,1,32]{2,1,0:T(1,128)S(1)}, u32[]{:S(2)}, u32[]{:S(2)}) async-start(f32[32,1,32]{2,1,0:T(1,128)} %get-tuple-element.312), calls=%async_computation.5 | async-start | bytes 32768 | tf_op jit(solution)/shard_map/all_to_all | solution.py:181
Sparse Core Ops, SparseCore 0:
  9.6 51.1 all-gather.1
where the time goes:
time: 199 us
  waiting for transfers between devices  103 us (52%)
  starting transfers between devices  20.5 us (10%)
  other arithmetic  20.3 us (10%)
  blocking collectives  14.8 us (7%)
  between operations  14.3 us (7%)
  matrix products  13.9 us (7%)
  local copies, waits for them, and re-layouts  11.7 us (6%)
    all_gather x1, waiting for transfers between devices, local(): image_rows = lax.all_gather(descriptors, 'grp', axis=0, tiled=True)  52.2 us
    all_to_all x1, waiting for transfers between devices, in_one_piece(): lax.all_to_all(both, axis, split_axis=split_dim, concat_axis=concat_dim,...  32.2 us
    all_to_all x1, blocking collectives, in_one_piece(): lax.all_to_all(both, axis, split_axis=split_dim, concat_axis=concat_dim,...  11.1 us
    reduce_sum x2, other arithmetic, first_pass(): jnp.sum(jnp.where(key_mask, jnp.exp(scores - row_top[:, None]), 0.0), axi...  9.7 us
    dot_general x2, matrix products, first_pass(): jnp.einsum('qd,kd->qk', block_rows, key_image, preferred_element_type=jnp...  7.9 us
    all_to_all x1, starting transfers between devices, in_one_piece(): lax.all_to_all(both, axis, split_axis=split_dim, concat_axis=concat_dim,...  7.87 us
    all_to_all x1, waiting for transfers between devices, paired_blocks(): lax.all_to_all(to_owner(row_out), TILE, split_axis=0, concat_axis=0, tile...  7.06 us
    all_to_all x1, waiting for transfers between devices, exchange_in_order(): out = lax.all_to_all(out, axes[k], k, k, tiled=True)  6.28 us
  transfers between devices with their start and end apart: 5, of which 5 were waited for; matrix products, arithmetic and copies ran while one was open for 3% of the time, Pallas kernels for 0%

commit v1 on v0

--- a/solution.py
+++ b/solution.py
@@ -194,7 +194,8 @@
 
 def local(descriptors, pairs, counts):
     score_scale = 2.0 / math.sqrt(descriptors.shape[2])
-    image_rows = lax.all_gather(descriptors, "grp", axis=0, tiled=True)
+    copies = jnp.concatenate([descriptors] * lax.axis_size("grp"), axis=0)
+    image_rows = lax.all_to_all(copies, "grp", 0, 0, tiled=True)
     image_ids = lax.iota(jnp.int32, counts.shape[0])
     first_image = pairs[:, 0]
     second = pairs[:, 1]

time: 199 us -> 192 us (0.965)
  between operations: 14.3 us -> 0.93 us
  starting transfers between devices: 20.5 us -> 27.5 us
  waiting for transfers between devices: 103 us -> 98.8 us
  other arithmetic: 20.3 us -> 23.7 us
    all_gather x1 -> x0, waiting for transfers between devices: 52.2 us -> none  [local(): image_rows = lax.all_gather(descriptors, 'grp', axis=0, tiled=True)]
    all_to_all x0 -> x1, waiting for transfers between devices: none -> 48.7 us  [local(): image_rows = lax.all_to_all(copies, 'grp', 0, 0, tiled=True)]
    all_to_all x0 -> x1, starting transfers between devices: none -> 4.99 us  [local(): image_rows = lax.all_to_all(copies, 'grp', 0, 0, tiled=True)]
    concatenate x0 -> x1, other arithmetic: none -> 4.19 us  [local(): copies = jnp.concatenate([descriptors] * lax.axis_size('grp'), axis=0)]
    all_to_all x1, starting transfers between devices: 7.87 us -> 9.97 us  [in_one_piece(): lax.all_to_all(both, axis, split_axis=split_dim, concat_axis=concat_dim,...]
  transfers between devices with their start and end apart: 5 -> 5, of which waited for: 5 -> 5; matrix products, arithmetic and copies ran while one was open for 3% -> 2% of each run, Pallas kernels for 0% -> 0%
where the time goes in v1:
time: 192 us; the launch traced here: 191 us
  waiting for transfers between devices  98.8 us (51%)
  starting transfers between devices  27.5 us (14%)
  other arithmetic  23.7 us (12%)
  blocking collectives  14.8 us (8%)
  matrix products  13.7 us (7%)
  local copies, waits for them, and re-layouts  11.6 us (6%)
    all_to_all x1, waiting for transfers between devices, local(): image_rows = lax.all_to_all(copies, 'grp', 0, 0, tiled=True)  48.7 us
    all_to_all x1, waiting for transfers between devices, in_one_piece(): lax.all_to_all(both, axis, split_axis=split_dim, concat_axis=concat_dim,...  32.2 us
    all_to_all x1, blocking collectives, in_one_piece(): lax.all_to_all(both, axis, split_axis=split_dim, concat_axis=concat_dim,...  11 us
    all_to_all x1, starting transfers between devices, in_one_piece(): lax.all_to_all(both, axis, split_axis=split_dim, concat_axis=concat_dim,...  9.97 us
    reduce_sum x2, other arithmetic, first_pass(): jnp.sum(jnp.where(key_mask, jnp.exp(scores - row_top[:, None]), 0.0), axi...  9.69 us
    dot_general x2, matrix products, first_pass(): jnp.einsum('qd,kd->qk', block_rows, key_image, preferred_element_type=jnp...  7.69 us
    all_to_all x1, waiting for transfers between devices, paired_blocks(): lax.all_to_all(to_owner(row_out), TILE, split_axis=0, concat_axis=0, tile...  7.06 us
    all_to_all x1, waiting for transfers between devices, exchange_in_order(): out = lax.all_to_all(out, axes[k], k, k, tiled=True)  6.28 us
  transfers between devices with their start and end apart: 5, of which 5 were waited for; matrix products, arithmetic and copies ran while one was open for 2% of the time, Pallas kernels for 0%

profile of v1, /device:TPU:1, one launch (start us, length us, event | category | flops | bytes accessed | tf_op | source)
XLA Modules:
  0.0 191.2 jit_solution(2028028431227697145)
XLA Ops:
  0.6 4.2 %pad_maximum_fusion = bf16[64,128,256]{2,1,0:T(8,128)(2,1)} fusion(bf16[16,128,256]{2,1,0:T(8,128)(2,1)} %param.9), kind=kLoop, calls=%fused_computation.24 | loop fusion | flops 6291456 | bytes 5242880 | tf_op jit(solution)/shard_map/concatenate | solution.py:197
  4.8 0.0 copy-start
  4.8 5.0 %all-to-all-start = ((bf16[64,128,256]{2,1,0:T(8,128)(2,1)}), bf16[64,128,256]{2,1,0:T(8,128)(2,1)}, u32[]{:S(2)}, u32[]{:S(2)}) async-start(bf16[64,128,256]{2,1,0:T(8,128)(2,1)} %pad_maximum_fusion), calls=%async_computation | async-start | bytes 8388608 | tf_op jit(solution)/shard_map/all_to_all | solution.py:198
  9.8 0.0 copy-done
  9.9 48.7 %all-to-all-done = bf16[64,128,256]{2,1,0:T(8,128)(2,1)} async-done(((bf16[64,128,256]{2,1,0:T(8,128)(2,1)}), bf16[64,128,256]{2,1,0:T(8,128)(2,1)}, u32[]{:S(2)}, u32[]{:S(2)}) %all-to-all-start) | async-done | bytes 4194336 | tf_op jit(solution)/shard_map/all_to_all | solution.py:198
  58.6 2.8 %gather_fusion = bf16[8,128,256]{2,1,0:T(8,128)(2,1)S(1)} fusion(bf16[64,128,256]{2,1,0:T(8,128)(2,1)} %all-to-all-done, s32[1024]{0:T(1024)S(1)} %pad_clamp_fusion.1), kind=kCustom, calls=%fused_computation.clone | custom fusion | bytes 1048608 | tf_op jit(solution)/shard_map/jit(_take)/gather | solution.py:208
  61.4 2.8 %gather_fusion.1 = bf16[8,128,256]{2,1,0:T(8,128)(2,1)S(1)} fusion(bf16[64,128,256]{2,1,0:T(8,128)(2,1)} %all-to-all-done, s32[1024]{0:T(1024)S(1)} %pad_clamp_fusion), kind=kCustom, calls=%fused_computation.1.clone | custom fusion | bytes 1048608 | tf_op jit(solution)/shard_map/jit(_take)/gather | solution.py:209
  64.1 0.2 broadcast_select_fusion
  64.3 0.2 broadcast_in_dim.140
  64.5 0.0 copy-start.1
  64.6 1.7 pad_maximum_fusion.1
  66.3 10.0 %all-to-all-start.1 = ((bf16[32,1,160,256]{3,2,1,0:T(8,128)(2,1)}), bf16[32,1,160,256]{3,2,1,0:T(8,128)(2,1)S(1)}, u32[]{:S(2)}, u32[]{:S(2)}) async-start(bf16[32,1,160,256]{3,2,1,0:T(8,128)(2,1)} %pad_maximum_fusion.1), calls=%async_computation.1 | async-start | bytes 5242880 | tf_op jit(solution)/shard_map/all_to_all | solution.py:16
  76.3 0.0 copy-done.1
  76.3 0.2 select_reduce_fusion.5
  76.5 0.6 dynamic_slice.52
  77.1 0.6 dynamic_slice.53
  77.7 0.1 add.159
  77.8 0.1 add.160
  77.9 0.1 add.162
  78.0 32.2 %all-to-all-done.1 = bf16[32,1,160,256]{3,2,1,0:T(8,128)(2,1)S(1)} async-done(((bf16[32,1,160,256]{3,2,1,0:T(8,128)(2,1)}), bf16[32,1,160,256]{3,2,1,0:T(8,128)(2,1)S(1)}, u32[]{:S(2)}, u32[]{:S(2)}) %all-to-all-start.1) | async-done | bytes 2621472 | tf_op jit(solution)/shard_map/all_to_all | solution.py:16
  110.2 1.5 slice.61
  111.7 20.4 %while.48 = (s32[]{:T(128)}, f32[4096]{0:T(1024)S(1)}, f32[4096]{0:T(1024)S(1)}, f32[2,512]{1,0:T(2,128)S(1)}, s32[2,512]{1,0:T(2,128)S(1)}, /*index=5*/s32[]{:T...) while((s32[]{:T(128)}, f32[4096]{0:T(1024)S(1)}, ...), condition=%wide.region_7.9_spmd.clone, body=%wide.region_2.8_spmd.clone.sunk | while | flops 1098936320 | bytes 19316360 | solution.py:86
  111.8 0.7 compare_reduce_fusion.8
  112.4 0.7 compare_reduce_fusion.7
  113.1 3.8 %select_reduce_fusion.11 = (f32[512]{0:T(512)S(1)}, f32[4096]{0:T(1024)S(1)}, f32[512,4096]{1,0:T(8,128)S(1)}) fusion(pred[4096]{0:T(1024)(128)(4,1)S(1)} %compare_reduce_fusion.7, pred[512]{0:T(512)(128)(4,1)S(1)} %compare_reduce_fusion.8, bf16[4096,256]{1,0:T(8,128)(2,1)} %get-tuple-element.457, bf16[2,512,256]{2,1,0:T(8,128)(2,1)S(1)} %get-tuple-element.456, ...), kind=kOutput, calls=%fused_computation.11.clone.1 | convolution fusion | flops 1084222976 | bytes 10770948 | tf_op jit(solution)/shard_map/while/body/eval_jaxpr/while/body/eval_jaxpr/qd,kd->qk/dot_general | solution.py:72
  117.0 4.8 %select_reduce_fusion.12 = (f32[512]{0:T(512)S(1)}, f32[4096]{0:T(1024)S(1)}) fusion(f32[512,4096]{1,0:T(8,128)S(1)} %get-tuple-element.421, f32[512]{0:T(512)S(1)} %get-tuple-element.422, pred[4096]{0:T(1024)(128)(4,1)S(1)} %compare_reduce_fusion.7, f32[4096]{0:T(1024)S(1)} %get-tuple-element.423, pred[512]{0:T(512)(128)(4,1)S(1)} %compare_reduce_fusion.8), kind=kLoop, calls=%fused_computation.10.clone.1 | loop fusion | flops 14675456 | bytes 8430080 | tf_op jit(solution)/shard_map/while/body/eval_jaxpr/while/body/eval_jaxpr/reduce_sum | solution.py:77
  121.9 0.7 compare_reduce_fusion.8
  122.6 0.7 compare_reduce_fusion.7
  123.3 3.8 %select_reduce_fusion.11 = (f32[512]{0:T(512)S(1)}, f32[4096]{0:T(1024)S(1)}, f32[512,4096]{1,0:T(8,128)S(1)}) fusion(pred[4096]{0:T(1024)(128)(4,1)S(1)} %compare_reduce_fusion.7, pred[512]{0:T(512)(128)(4,1)S(1)} %compare_reduce_fusion.8, bf16[4096,256]{1,0:T(8,128)(2,1)} %get-tuple-element.457, bf16[2,512,256]{2,1,0:T(8,128)(2,1)S(1)} %get-tuple-element.456, ...), kind=kOutput, calls=%fused_computation.11.clone.1 | convolution fusion | flops 1084222976 | bytes 10770948 | tf_op jit(solution)/shard_map/while/body/eval_jaxpr/while/body/eval_jaxpr/qd,kd->qk/dot_general | solution.py:72
  127.2 4.8 %select_reduce_fusion.12 = (f32[512]{0:T(512)S(1)}, f32[4096]{0:T(1024)S(1)}) fusion(f32[512,4096]{1,0:T(8,128)S(1)} %get-tuple-element.421, f32[512]{0:T(512)S(1)} %get-tuple-element.422, pred[4096]{0:T(1024)(128)(4,1)S(1)} %compare_reduce_fusion.7, f32[4096]{0:T(1024)S(1)} %get-tuple-element.423, pred[512]{0:T(512)(128)(4,1)S(1)} %compare_reduce_fusion.8), kind=kLoop, calls=%fused_computation.10.clone.1 | loop fusion | flops 14675456 | bytes 8430080 | tf_op jit(solution)/shard_map/while/body/eval_jaxpr/while/body/eval_jaxpr/reduce_sum | solution.py:77
  132.2 11.0 %all_to_all.35 = f32[32,2,128]{2,1,0:T(2,128)S(1)} all-to-all(f32[32,2,128]{2,1,0:T(2,128)S(1)} %pad_maximum_fusion.2), channel_id=1, replica_groups=mesh['grp'=4,'tile_0'=4,'tile_1'=4,'tile_2'=2] {'tile_0','tile_1','tile_2'}, dimensions={0} | all-to-all | bytes 65536 | tf_op jit(solution)/shard_map/all_to_all | solution.py:16
  143.3 3.8 %all_to_all.36 = f32[16,2,1,1,128]{4,3,2,0,1:T(1,128)S(1)} all-to-all(f32[16,2,1,1,128]{4,3,2,0,1:T(1,128)S(1)} %broadcast_in_dim.147), channel_id=1, replica_groups=mesh['grp'=4,'tile_0'=4,'tile_1'=4,'tile_2'=2] {'tile_2'}, dimensions={1} | all-to-all | bytes 32768 | tf_op jit(solution)/shard_map/all_to_all | solution.py:42
  147.1 0.6 copy.102
  147.7 3.5 %all-to-all-start.5 = ((f32[16,2,1,1,128]{4,3,2,1,0:T(1,128)}), f32[16,2,1,1,128]{4,3,2,1,0:T(1,128)S(1)}, u32[]{:S(2)}, u32[]{:S(2)}) async-start(f32[16,2,1,1,128]{4,3,2,1,0:T(1,128)} %copy.102), calls=%async_computation.5 | async-start | bytes 32768 | tf_op jit(solution)/shard_map/all_to_all | solution.py:42
  151.2 0.1 squeeze.81
  151.3 6.3 %all-to-all-done.5 = f32[16,2,1,1,128]{4,3,2,1,0:T(1,128)S(1)} async-done(((f32[16,2,1,1,128]{4,3,2,1,0:T(1,128)}), f32[16,2,1,1,128]{4,3,2,1,0:T(1,128)S(1)}, u32[]{:S(2)}, u32[]{:S(2)}) %all-to-all-start.5) | async-done | bytes 16416 | tf_op jit(solution)/shard_map/all_to_all | solution.py:42
  157.6 7.6 %while.47 = (s32[]{:T(128)}, f32[2,512]{1,0:T(2,128)S(1)}, bf16[2,512,256]{2,1,0:T(8,128)(2,1)S(1)}, bf16[4096,256]{1,0:T(8,128)(2,1)}, f32[4096]{0:T(1024)S(1)}...) while((s32[]{:T(128)}, f32[2,512]{1,0:T(2,128)S(1)}, ...), condition=%wide.region_10.12_spmd.clone, body=%wide.region_8.11_spmd.clone.sunk | while | flops 1082134528 | bytes 2396269 | solution.py:113
  157.6 0.7 compare_reduce_fusion.6
  158.3 3.0 %select_reduce_fusion.10 = f32[512]{0:T(512)S(1)} fusion(bf16[4096,256]{1,0:T(8,128)(2,1)} %get-tuple-element.482, f32[4096]{0:T(1024)S(1)} %get-tuple-element.483, pred[4096]{0:T(1024)(128)(4,1)S(1)} %compare_reduce_fusion.6, bf16[2,512,256]{2,1,0:T(8,128)(2,1)S(1)} %get-tuple-element.481, s32[]{:T(128)} %get-tuple-element.470), kind=kOutput, calls=%fused_computation.4.clone.1 | convolution fusion | flops 1082129920 | bytes 2381828 | tf_op jit(solution)/shard_map/while/body/eval_jaxpr/while/body/eval_jaxpr/qd,kd->qk/dot_general | solution.py:104
  161.4 0.7 compare_reduce_fusion.6
  162.1 3.0 %select_reduce_fusion.10 = f32[512]{0:T(512)S(1)} fusion(bf16[4096,256]{1,0:T(8,128)(2,1)} %get-tuple-element.482, f32[4096]{0:T(1024)S(1)} %get-tuple-element.483, pred[4096]{0:T(1024)(128)(4,1)S(1)} %compare_reduce_fusion.6, bf16[2,512,256]{2,1,0:T(8,128)(2,1)S(1)} %get-tuple-element.481, s32[]{:T(128)} %get-tuple-element.470), kind=kOutput, calls=%fused_computation.4.clone.1 | convolution fusion | flops 1082129920 | bytes 2381828 | tf_op jit(solution)/shard_map/while/body/eval_jaxpr/while/body/eval_jaxpr/qd,kd->qk/dot_general | solution.py:104
  165.2 0.1 reshape.246
  165.3 1.4 compare_select_fusion
  166.6 4.9 %all-to-all-start.2 = ((f32[32,1,32]{2,1,0:T(1,128)}), f32[32,1,32]{2,1,0:T(1,128)S(1)}, u32[]{:S(2)}, u32[]{:S(2)}) async-start(f32[32,1,32]{2,1,0:T(1,128)} %get-tuple-element.313), calls=%async_computation.2 | async-start | bytes 32768 | tf_op jit(solution)/shard_map/all_to_all | solution.py:180
  171.6 7.1 %all-to-all-done.2 = f32[32,1,32]{2,1,0:T(1,128)S(1)} async-done(((f32[32,1,32]{2,1,0:T(1,128)}), f32[32,1,32]{2,1,0:T(1,128)S(1)}, u32[]{:S(2)}, u32[]{:S(2)}) %all-to-all-start.2) | async-done | bytes 4128 | tf_op jit(solution)/shard_map/all_to_all | solution.py:180
  178.6 4.2 %all-to-all-start.6 = ((f32[32,1,32]{2,1,0:T(1,128)}), f32[32,1,32]{2,1,0:T(1,128)S(1)}, u32[]{:S(2)}, u32[]{:S(2)}) async-start(f32[32,1,32]{2,1,0:T(1,128)} %get-tuple-element.312), calls=%async_computation.6 | async-start | bytes 32768 | tf_op jit(solution)/shard_map/all_to_all | solution.py:181
  182.8 0.7 add_select_fusion
  183.4 0.5 broadcast.199
  184.0 0.7 reduce.12
  184.6 0.7 reshape_transpose_reshape.10
  185.3 4.5 %all-to-all-done.6 = f32[32,1,32]{2,1,0:T(1,128)S(1)} async-done(((f32[32,1,32]{2,1,0:T(1,128)}), f32[32,1,32]{2,1,0:T(1,128)S(1)}, u32[]{:S(2)}, u32[]{:S(2)}) %all-to-all-start.6) | async-done | bytes 4128 | tf_op jit(solution)/shard_map/all_to_all | solution.py:181
  189.9 0.7 reduce.13
  190.6 0.7 reshape_transpose_reshape.11
  (31 shorter events, 0.5 us)
Async XLA Ops:
  4.8 5.0 %copy-start = (s32[8,2]{0,1:T(2,128)S(1)}, s32[8,2]{0,1:T(2,128)}, u32[]{:S(2)}) copy-start(s32[8,2]{0,1:T(2,128)} %param.10) | copy-start | bytes 196
  4.8 53.8 %all-to-all-start = ((bf16[64,128,256]{2,1,0:T(8,128)(2,1)}), bf16[64,128,256]{2,1,0:T(8,128)(2,1)}, u32[]{:S(2)}, u32[]{:S(2)}) async-start(bf16[64,128,256]{2,1,0:T(8,128)(2,1)} %pad_maximum_fusion), calls=%async_computation | async-start | bytes 8388608 | tf_op jit(solution)/shard_map/all_to_all | solution.py:198
  64.5 11.8 %copy-start.1 = (s32[64]{0:T(128)S(1)}, s32[64]{0:T(128)}, u32[]{:S(2)}) copy-start(s32[64]{0:T(128)} %param.11) | copy-start | bytes 772
  66.3 43.9 %all-to-all-start.1 = ((bf16[32,1,160,256]{3,2,1,0:T(8,128)(2,1)}), bf16[32,1,160,256]{3,2,1,0:T(8,128)(2,1)S(1)}, u32[]{:S(2)}, u32[]{:S(2)}) async-start(bf16[32,1,160,256]{3,2,1,0:T(8,128)(2,1)} %pad_maximum_fusion.1), calls=%async_computation.1 | async-start | bytes 5242880 | tf_op jit(solution)/shard_map/all_to_all | solution.py:16
  147.7 9.9 %all-to-all-start.5 = ((f32[16,2,1,1,128]{4,3,2,1,0:T(1,128)}), f32[16,2,1,1,128]{4,3,2,1,0:T(1,128)S(1)}, u32[]{:S(2)}, u32[]{:S(2)}) async-start(f32[16,2,1,1,128]{4,3,2,1,0:T(1,128)} %copy.102), calls=%async_computation.5 | async-start | bytes 32768 | tf_op jit(solution)/shard_map/all_to_all | solution.py:42
  166.6 12.0 %all-to-all-start.2 = ((f32[32,1,32]{2,1,0:T(1,128)}), f32[32,1,32]{2,1,0:T(1,128)S(1)}, u32[]{:S(2)}, u32[]{:S(2)}) async-start(f32[32,1,32]{2,1,0:T(1,128)} %get-tuple-element.313), calls=%async_computation.2 | async-start | bytes 32768 | tf_op jit(solution)/shard_map/all_to_all | solution.py:180
  178.6 11.2 %all-to-all-start.6 = ((f32[32,1,32]{2,1,0:T(1,128)}), f32[32,1,32]{2,1,0:T(1,128)S(1)}, u32[]{:S(2)}, u32[]{:S(2)}) async-start(f32[32,1,32]{2,1,0:T(1,128)} %get-tuple-element.312), calls=%async_computation.6 | async-start | bytes 32768 | tf_op jit(solution)/shard_map/all_to_all | solution.py:181
